TPU v7x, 32 devices: a whole 2x2x4 slice. The times are simulated.
32 devices in a mesh: dp: 8 (over y, x, core), mp: 4 (over z).
Axes of the slice: x: 2, y: 2, z: 4, core: 2. Of those that a mesh axis runs over, the one named last changes fastest.
Arguments:
- hidden_in: float32 [16384, 768], P(('dp', 'mp')), may hold values from -6 to 6
- first_values: bfloat16 [16384, 384], P('dp', 'mp'), may hold values from -6 to 6
- first_length: int32 [8], P('dp'), may hold values from 1024 to 2048, as said below
- pre_gain: float32 [768], replicated, may hold values from 0.25 to 1.75
- pre_shift: float32 [768], replicated, may hold values from -1.75 to 1.75
- w_query: bfloat16 [768, 768], P(None, 'mp'), may hold values from -0.21875 to 0.21875
- b_query: float32 [768], P('mp'), may hold values from -3 to 3
- w_key: bfloat16 [768, 768], P(None, 'mp'), may hold values from -0.21875 to 0.21875
- w_value: bfloat16 [768, 384], P(None, 'mp'), may hold values from -0.21875 to 0.21875
- b_value: float32 [384], P('mp'), may hold values from -3 to 3
- w_out: bfloat16 [768, 768], P('mp'), may hold values from -1.75 to 1.75
- b_out: float32 [768], replicated, may hold values from -3 to 3
- mid_gain: float32 [768], replicated, may hold values from 0.25 to 1.75
- mid_shift: float32 [768], replicated, may hold values from -1.75 to 1.75
- w_up: bfloat16 [768, 3072], P(None, 'mp'), may hold values from -0.21875 to 0.21875
- b_up: float32 [3072], P('mp'), may hold values from -3 to 3
- w_down: bfloat16 [3072, 768], P('mp'), may hold values from -0.109375 to 0.109375
- b_down: float32 [768], replicated, may hold values from -3 to 3
- grad_out: float32 [16384, 768], P(('dp', 'mp')), may hold values from -6 to 6
Outputs:
- layer_out: float32 [16384, 768], P(('dp', 'mp'))
- grad_in: float32 [16384, 768], P(('dp', 'mp'))
- grad_first_values: float32 [16384, 384], P('dp', 'mp')
- grad_pre_gain: float32 [768], replicated
- grad_pre_shift: float32 [768], replicated
- grad_w_query: float32 [768, 768], P(None, 'mp')
- grad_b_query: float32 [768], P('mp')
- grad_w_key: float32 [768, 768], P(None, 'mp')
- grad_w_value: float32 [768, 384], P(None, 'mp')
- grad_b_value: float32 [384], P('mp')
- grad_w_out: float32 [768, 768], P('mp')
- grad_b_out: float32 [768], replicated
- grad_mid_gain: float32 [768], replicated
- grad_mid_shift: float32 [768], replicated
- grad_w_up: float32 [768, 3072], P(None, 'mp')
- grad_b_up: float32 [3072], P('mp')
- grad_w_down: float32 [3072, 768], P('mp')
- grad_b_down: float32 [768], replicated
Inputs may be any that keep to these rules, and one draw needn't show every extreme that they name: `first_length`: each entry is 2048 / 2 (two documents in the block) or 2048 (one document); half of the entries take each value.
All inputs are finite; a program needn't handle non-finite values.
Results may differ from a plain program's by a relative error of at most 0.02.
Values may be sent and summed in bfloat16 or wider, within the bound.
A program may use at most 192 MiB of HBM per device.

v0:
```python
import jax
import jax.numpy as jnp
from jax import lax
from jax.sharding import PartitionSpec as P

HEAD_DIM = 64


EPSILON = 1e-05
NEG_LARGE = -1e30


def layer_norm(values, gain, shift):
    center = values - jnp.mean(values, -1, keepdims=True)
    spread = jnp.mean(center * center, -1, keepdims=True)
    return center * lax.rsqrt(spread + EPSILON) * gain + shift


def gelu_tanh(values):
    return (
        0.5
        * values
        * (1.0 + jnp.tanh(0.7978845608028654 * (values + 0.044715 * values * values * values)))
    )


def product(left, right):
    return jnp.dot(left, right, preferred_element_type=jnp.float32)


def product_left_t(left, right):
    return lax.dot_general(
        left, right, (((0,), (0,)), ((), ())), preferred_element_type=jnp.float32
    )


def product_right_t(left, right):
    return lax.dot_general(
        left, right, (((1,), (1,)), ((), ())), preferred_element_type=jnp.float32
    )


def block_scores(query_rows, keys_all, key_block, query_block, size, boundary, scale):
    key_rows = lax.dynamic_slice_in_dim(keys_all, key_block * size, size, 0)
    scores = (
        jnp.einsum("qhd,khd->hqk", query_rows, key_rows, preferred_element_type=jnp.float32) * scale
    )
    query_pos = query_block * size + jnp.arange(size, dtype=jnp.int32)
    key_pos = key_block * size + jnp.arange(size, dtype=jnp.int32)
    same_doc = (query_pos[:, None] >= boundary) == (key_pos[None, :] >= boundary)
    allowed = (key_pos[None, :] <= query_pos[:, None]) & same_doc
    return jnp.where(allowed[None], scores, NEG_LARGE)


def lowest_block(query_block, size, boundary):
    return jnp.where(query_block * size >= boundary, boundary // size, 0)


def attend_forward(queries, keys_all, values_all, boundary, scale):
    count, heads_here, head_dim = queries.shape
    size = min(512, count // 2)
    contexts = []
    exact_contexts = []
    totals = []
    for query_block in range(count // size):
        query_rows = queries[query_block * size : (query_block + 1) * size]
        lowest = lowest_block(query_block, size, boundary)

        def online_step(key_block, carry):
            run_max, run_sum, running = carry
            scores = block_scores(
                query_rows, keys_all, key_block, query_block, size, boundary, scale
            )
            new_max = jnp.maximum(run_max, jnp.max(scores, -1))
            factor = jnp.exp(run_max - new_max)
            weights = jnp.exp(scores - new_max[..., None])
            run_sum = run_sum * factor + jnp.sum(weights, -1)
            value_rows = lax.dynamic_slice_in_dim(values_all, key_block * size, size, 0)
            running = running * jnp.transpose(factor)[..., None] + jnp.einsum(
                "hqk,khd->qhd",
                weights.astype(jnp.bfloat16),
                value_rows,
                preferred_element_type=jnp.float32,
            )
            return (new_max, run_sum, running)

        start_max = jnp.full((heads_here, size), NEG_LARGE, jnp.float32)
        start_sum = jnp.zeros((heads_here, size), jnp.float32)
        start_run = jnp.zeros((size, heads_here, head_dim), jnp.float32)
        run_max, run_sum, running = lax.fori_loop(
            lowest, query_block + 1, online_step, (start_max, start_sum, start_run)
        )
        log_total = run_max + jnp.log(run_sum)
        context = running / jnp.transpose(run_sum)[..., None]
        exact_contexts.append(context)
        contexts.append(context.reshape(size, heads_here * head_dim).astype(jnp.bfloat16))
        totals.append(log_total)
    return (
        jnp.concatenate(contexts, 0),
        jnp.concatenate(totals, 1),
        jnp.concatenate(exact_contexts, 0),
    )


def attend_backward(
    queries, keys_all, values_all, grad_context, exact_context, log_totals, boundary, scale
):
    count, heads_here, head_dim = queries.shape
    size = min(512, count // 2)
    grad_keys = jnp.zeros((count, heads_here, head_dim), jnp.float32)
    grad_values = jnp.zeros((count, heads_here, head_dim), jnp.float32)
    grad_queries = []
    for query_block in range(count // size):
        query_rows = queries[query_block * size : (query_block + 1) * size]
        grad_rows = grad_context[query_block * size : (query_block + 1) * size]
        context_rows = exact_context[query_block * size : (query_block + 1) * size]
        log_total = log_totals[:, query_block * size : (query_block + 1) * size]
        lowest = lowest_block(query_block, size, boundary)
        delta = jnp.transpose(jnp.sum(grad_rows.astype(jnp.float32) * context_rows, -1))

        def add_grads(key_block, carry):
            grad_q, grad_k, grad_v = carry
            scores = block_scores(
                query_rows, keys_all, key_block, query_block, size, boundary, scale
            )
            probabilities = jnp.exp(scores - log_total[..., None])
            value_rows = lax.dynamic_slice_in_dim(values_all, key_block * size, size, 0)
            grad_probs = jnp.einsum(
                "qhd,khd->hqk", grad_rows, value_rows, preferred_element_type=jnp.float32
            )
            grad_scores = (probabilities * (grad_probs - delta[..., None])).astype(jnp.bfloat16)
            key_rows = lax.dynamic_slice_in_dim(keys_all, key_block * size, size, 0)
            grad_q = (
                grad_q
                + jnp.einsum(
                    "hqk,khd->qhd", grad_scores, key_rows, preferred_element_type=jnp.float32
                )
                * scale
            )
            key_part = (
                jnp.einsum(
                    "hqk,qhd->khd", grad_scores, query_rows, preferred_element_type=jnp.float32
                )
                * scale
            )
            value_part = jnp.einsum(
                "hqk,qhd->khd",
                probabilities.astype(jnp.bfloat16),
                grad_rows,
                preferred_element_type=jnp.float32,
            )
            start = key_block * size
            grad_k = lax.dynamic_update_slice_in_dim(
                grad_k, lax.dynamic_slice_in_dim(grad_k, start, size, 0) + key_part, start, 0
            )
            grad_v = lax.dynamic_update_slice_in_dim(
                grad_v, lax.dynamic_slice_in_dim(grad_v, start, size, 0) + value_part, start, 0
            )
            return (grad_q, grad_k, grad_v)

        start_q = jnp.zeros((size, heads_here, head_dim), jnp.float32)
        grad_q, grad_keys, grad_values = lax.fori_loop(
            lowest, query_block + 1, add_grads, (start_q, grad_keys, grad_values)
        )
        grad_queries.append(grad_q)
    return (jnp.concatenate(grad_queries, 0), grad_keys, grad_values)


def shards(
    hidden_in,
    first_values,
    first_length,
    pre_gain,
    pre_shift,
    w_query,
    b_query,
    w_key,
    w_value,
    b_value,
    w_out,
    b_out,
    mid_gain,
    mid_shift,
    w_up,
    b_up,
    w_down,
    b_down,
    grad_out,
):
    model_rank = lax.axis_index("mp")
    model_count = lax.axis_size("mp")
    boundary = first_length[0]
    head_width = w_query.shape[1]
    heads_here = head_width // HEAD_DIM
    scale = HEAD_DIM ** (-0.5)
    normed_local = layer_norm(hidden_in, pre_gain, pre_shift).astype(jnp.bfloat16)
    normed = lax.all_gather(normed_local, "mp", axis=0, tiled=True)
    count = normed.shape[0]
    queries = (product(normed, w_query) + b_query).astype(jnp.bfloat16)
    keys_all = product(normed, w_key).astype(jnp.bfloat16)
    fresh_values = (product(normed, w_value) + b_value).astype(jnp.bfloat16)
    piece_width = fresh_values.shape[1]
    pieces_used = head_width // piece_width
    sources = []
    for which in range(pieces_used):
        number = model_rank * pieces_used + which
        sources.append(jnp.where(number < model_count, number, number - model_count))
    fresh_all, reused_all = (
        lax.all_gather(fresh_values, "mp", axis=1, tiled=True),
        lax.all_gather(first_values, "mp", axis=1, tiled=True),
    )
    fresh_width = fresh_all.shape[1]
    value_source = jnp.concatenate([fresh_all, reused_all], 1)
    values_all = lax.dynamic_slice_in_dim(value_source, model_rank * head_width, head_width, 1)
    query_heads = queries.reshape(count, heads_here, HEAD_DIM)
    key_heads = keys_all.reshape(count, heads_here, HEAD_DIM)
    value_heads = values_all.reshape(count, heads_here, HEAD_DIM)
    context, log_totals, exact_context = attend_forward(
        query_heads, key_heads, value_heads, boundary, scale
    )
    piece = context
    attended = (
        lax.psum_scatter(
            product(piece, w_out).astype(jnp.bfloat16), "mp", scatter_dimension=0, tiled=True
        ).astype(jnp.float32)
        + b_out
    )
    middle = hidden_in + attended
    normed_mid_local = layer_norm(middle, mid_gain, mid_shift).astype(jnp.bfloat16)
    grad_down = grad_out.astype(jnp.bfloat16)
    normed_mid, grad_down_all = (
        lax.all_gather(normed_mid_local, "mp", axis=0, tiled=True),
        lax.all_gather(grad_down, "mp", axis=0, tiled=True),
    )
    up_values = product(normed_mid, w_up) + b_up
    activated = gelu_tanh(up_values).astype(jnp.bfloat16)
    piece = activated
    layer_out = middle + (
        lax.psum_scatter(
            product(piece, w_down).astype(jnp.bfloat16), "mp", scatter_dimension=0, tiled=True
        ).astype(jnp.float32)
        + b_down
    )
    grad_b_down = jnp.sum(grad_down.astype(jnp.float32), 0)
    grad_w_down = product_left_t(activated, grad_down_all)
    grad_activated = product_right_t(grad_down_all, w_down)
    _, gelu_pull = jax.vjp(gelu_tanh, up_values)
    grad_up = gelu_pull(grad_activated)[0].astype(jnp.bfloat16)
    grad_w_up = product_left_t(normed_mid, grad_up)
    grad_b_up = jnp.sum(grad_up.astype(jnp.float32), 0)
    piece = grad_up
    grad_normed_mid = lax.psum_scatter(
        product_right_t(piece, w_up).astype(jnp.bfloat16), "mp", scatter_dimension=0, tiled=True
    ).astype(jnp.float32)
    _, mid_pull = jax.vjp(layer_norm, middle, mid_gain, mid_shift)
    grad_mid_part, grad_mid_gain, grad_mid_shift = mid_pull(grad_normed_mid)
    grad_middle = grad_out + grad_mid_part
    grad_attn = grad_middle.astype(jnp.bfloat16)
    grad_b_out = jnp.sum(grad_attn.astype(jnp.float32), 0)
    grad_attn_all = lax.all_gather(grad_attn, "mp", axis=0, tiled=True)
    grad_w_out = product_left_t(context, grad_attn_all)
    grad_context = product_right_t(grad_attn_all, w_out).astype(jnp.bfloat16)
    grad_q, grad_k, grad_v = attend_backward(
        query_heads,
        key_heads,
        value_heads,
        grad_context.reshape(count, heads_here, HEAD_DIM),
        exact_context,
        log_totals,
        boundary,
        scale,
    )
    grad_queries = grad_q.reshape(count, head_width).astype(jnp.bfloat16)
    grad_keys = grad_k.reshape(count, head_width).astype(jnp.bfloat16)
    grad_value_cols = grad_v.reshape(count, head_width)
    placed = jnp.zeros((count, value_source.shape[1]), jnp.float32)
    placed = lax.dynamic_update_slice_in_dim(placed, grad_value_cols, model_rank * head_width, 1)
    grad_fresh, grad_first = (
        lax.psum_scatter(
            placed[:, :fresh_width].astype(jnp.bfloat16), "mp", scatter_dimension=1, tiled=True
        ).astype(jnp.float32),
        lax.psum_scatter(
            placed[:, fresh_width:].astype(jnp.bfloat16), "mp", scatter_dimension=1, tiled=True
        ).astype(jnp.float32),
    )
    grad_fresh = grad_fresh.astype(jnp.bfloat16)
    grad_w_query = product_left_t(normed, grad_queries)
    grad_b_query = jnp.sum(grad_queries.astype(jnp.float32), 0)
    grad_w_key = product_left_t(normed, grad_keys)
    grad_w_value = product_left_t(normed, grad_fresh)
    grad_b_value = jnp.sum(grad_fresh.astype(jnp.float32), 0)
    grad_normed = lax.psum_scatter(
        (
            product_right_t(grad_queries, w_query)
            + product_right_t(grad_keys, w_key)
            + product_right_t(grad_fresh, w_value)
        ).astype(jnp.bfloat16),
        "mp",
        scatter_dimension=0,
        tiled=True,
    ).astype(jnp.float32)
    _, pre_pull = jax.vjp(layer_norm, hidden_in, pre_gain, pre_shift)
    grad_pre_part, grad_pre_gain, grad_pre_shift = pre_pull(grad_normed)
    grad_input = grad_middle + grad_pre_part
    rest_w_up, rest_b_up, rest_w_down = (grad_w_up, grad_b_up, grad_w_down)
    (
        grad_w_query,
        grad_b_query,
        grad_w_key,
        grad_w_value,
        grad_b_value,
        grad_w_out,
        rest_w_up,
        rest_b_up,
        rest_w_down,
    ) = lax.psum(
        (
            grad_w_query,
            grad_b_query,
            grad_w_key,
            grad_w_value,
            grad_b_value,
            grad_w_out,
            rest_w_up,
            rest_b_up,
            rest_w_down,
        ),
        "dp",
    )
    grad_w_up, grad_b_up, grad_w_down = (rest_w_up, rest_b_up, rest_w_down)
    grad_pre_gain, grad_pre_shift, grad_b_out, grad_mid_gain, grad_mid_shift, grad_b_down = (
        lax.psum(
            (grad_pre_gain, grad_pre_shift, grad_b_out, grad_mid_gain, grad_mid_shift, grad_b_down),
            ("dp", "mp"),
        )
    )
    return (
        layer_out,
        grad_input,
        grad_first,
        grad_pre_gain,
        grad_pre_shift,
        grad_w_query,
        grad_b_query,
        grad_w_key,
        grad_w_value,
        grad_b_value,
        grad_w_out,
        grad_b_out,
        grad_mid_gain,
        grad_mid_shift,
        grad_w_up,
        grad_b_up,
        grad_w_down,
        grad_b_down,
    )


def solution(mesh):
    placed = (
        P(("dp", "mp"), None),
        P("dp", "mp"),
        P("dp"),
        P(),
        P(),
        P(None, "mp"),
        P("mp"),
        P(None, "mp"),
        P(None, "mp"),
        P("mp"),
        P("mp", None),
        P(),
        P(),
        P(),
        P(None, "mp"),
        P("mp"),
        P("mp", None),
        P(),
        P(("dp", "mp"), None),
    )
    return jax.shard_map(
        shards,
        mesh=mesh,
        in_specs=placed,
        out_specs=(
            P(("dp", "mp"), None),
            P(("dp", "mp"), None),
            P("dp", "mp"),
            P(),
            P(),
            P(None, "mp"),
            P("mp"),
            P(None, "mp"),
            P(None, "mp"),
            P("mp"),
            P("mp", None),
            P(),
            P(),
            P(),
            P(None, "mp"),
            P("mp"),
            P("mp", None),
            P(),
        ),
        check_vma=False,
    )
```

profile of v0, /device:TPU:0, one launch (start us, length us, event | category | flops | bytes accessed | tf_op | source)
XLA Modules:
  0.0 987.2 jit_solution(6944280624142588855)
XLA Ops:
  12.8 65.5 %all-gather.7.cloned.1.call-done = bf16[2048,768]{1,0:T(8,128)(2,1)} async-done(((bf16[512,768]{1,0:T(8,128)(2,1)}), bf16[2048,768]{1,0:T(8,128)(2,1)}) %all-gather.7.cloned.1.call-update) | async-done | bytes 3145744 | tf_op jit(solution)/shard_map/all_gather | solution.py:197
  88.2 27.5 %all-gather.11.cloned.1.call-done = bf16[2048,384]{0,1:T(8,128)(2,1)} async-done(((bf16[2048,96]{0,1:T(8,128)(2,1)}), bf16[2048,384]{0,1:T(8,128)(2,1)}) %all-gather.11.cloned.1.call-update) | async-done | bytes 1572880 | tf_op jit(solution)/shard_map/all_gather | solution.py:210
  115.7 38.1 %all-gather.9.cloned.1.call-done = bf16[2048,384]{0,1:T(8,128)(2,1)} async-done(((bf16[2048,96]{0,1:T(8,128)(2,1)}), bf16[2048,384]{0,1:T(8,128)(2,1)}) %all-gather.9.cloned.1.call-update) | async-done | bytes 1572880 | tf_op jit(solution)/shard_map/all_gather | solution.py:209
  157.6 24.8 %while.115 = (s32[]{:T(128)}, f32[3,512]{1,0:T(4,128)S(1)}, f32[3,512]{1,0:T(4,128)}, f32[512,3,64]{0,2,1:T(8,128)}, s32[]{:T(128)}, /*index=5*/bf16[2048,3,64]{...) while((s32[]{:T(128)}, f32[3,512]{1,0:T(4,128)S(1)}, ...), condition=%wide.region_17.18_spmd, body=%wide.region_14.17_spmd.sunk | while | flops 210968064 | bytes 15165735 | solution.py:90
  183.8 18.6 %while.114 = (s32[]{:T(128)}, f32[3,512]{1,0:T(4,128)S(1)}, f32[3,512]{1,0:T(4,128)}, f32[512,3,64]{0,2,1:T(8,128)}, s32[]{:T(128)}, /*index=5*/bf16[2048,3,64]{...) while((s32[]{:T(128)}, f32[3,512]{1,0:T(4,128)S(1)}, ...), condition=%wide.region_13.14_spmd, body=%wide.region_10.13_spmd.sunk | while | flops 210968064 | bytes 15165735 | solution.py:90
  204.3 12.4 %while.113 = (s32[]{:T(128)}, f32[3,512]{1,0:T(4,128)}, f32[3,512]{1,0:T(4,128)}, f32[512,3,64]{0,2,1:T(8,128)}, s32[]{:T(128)}, /*index=5*/bf16[2048,3,64]{0,2,...) while((s32[]{:T(128)}, f32[3,512]{1,0:T(4,128)}, ...), condition=%wide.region_9.10_spmd, body=%wide.region_6.9_spmd.sunk | while | flops 210968064 | bytes 15190339 | solution.py:90
  233.3 59.4 %reduce-scatter.7.cloned.1.call-done = bf16[512,768]{1,0:T(8,128)(2,1)} async-done(((bf16[2048,768]{1,0:T(8,128)(2,1)}), bf16[512,768]{1,0:T(8,128)(2,1)}) %reduce-scatter.7.cloned.1.call-update) | async-done | bytes 786448 | tf_op jit(solution)/shard_map/reduce_scatter | solution.py:223
  298.8 61.8 %all-gather.13.cloned.1.call-done = bf16[2048,768]{1,0:T(8,128)(2,1)} async-done(((bf16[512,768]{1,0:T(8,128)(2,1)}), bf16[2048,768]{1,0:T(8,128)(2,1)}) %all-gather.13.cloned.1.call-update) | async-done | bytes 3145744 | tf_op jit(solution)/shard_map/all_gather | solution.py:232
  360.6 7.5 fusion.237
  368.1 56.6 %all-gather.15.cloned.1.call-done = bf16[2048,768]{1,0:T(8,128)(2,1)} async-done(((bf16[512,768]{1,0:T(8,128)(2,1)}), bf16[2048,768]{1,0:T(8,128)(2,1)}) %all-gather.15.cloned.1.call-update) | async-done | bytes 3145744 | tf_op jit(solution)/shard_map/all_gather | solution.py:233
  424.7 12.1 %convert_reduce_fusion = (f32[768]{0:T(1024)}, bf16[2048,768]{1,0:T(8,128)(2,1)S(1)}, bf16[2048,768]{1,0:T(8,128)(2,1)}) fusion(f32[2048,768]{1,0:T(8,128)} %fusion.237, f32[768]{0:T(1024)S(1)} %copy-done.115, bf16[2048,768]{1,0:T(8,128)(2,1)} %all-gather.15.cloned.1.call-done, bf16[768,768]{1,0:T(8,128)(2,1)S(1)} %copy-done), kind=kOutput, calls=%fused_computation.234 | convolution fusion | flops 2461531392 | bytes 16914432 | tf_op jit(solution)/shard_map/dot_general | solution.py:38
  449.3 52.5 %reduce-scatter.11.cloned.1.call-done = bf16[512,768]{1,0:T(8,128)(2,1)} async-done(((bf16[2048,768]{1,0:T(8,128)(2,1)}), bf16[512,768]{1,0:T(8,128)(2,1)}) %reduce-scatter.11.cloned.1.call-update) | async-done | bytes 786448 | tf_op jit(solution)/shard_map/reduce_scatter | solution.py:252
  504.1 60.2 %reduce-scatter.9.cloned.1.call-done = bf16[512,768]{1,0:T(8,128)(2,1)} async-done(((bf16[2048,768]{1,0:T(8,128)(2,1)}), bf16[512,768]{1,0:T(8,128)(2,1)}) %reduce-scatter.9.cloned.1.call-update) | async-done | bytes 786448 | tf_op jit(solution)/shard_map/reduce_scatter | solution.py:239
  572.1 61.0 %all-gather.17.cloned.1.call-done = bf16[2048,768]{1,0:T(8,128)(2,1)} async-done(((bf16[512,768]{1,0:T(8,128)(2,1)}), bf16[2048,768]{1,0:T(8,128)(2,1)}) %all-gather.17.cloned.1.call-update) | async-done | bytes 3145744 | tf_op jit(solution)/shard_map/all_gather | solution.py:260
  639.4 7.6 while.116
  647.1 15.4 %while.117 = (s32[]{:T(128)}, f32[512,3,64]{0,2,1:T(8,128)S(1)}, f32[2048,3,64]{0,2,1:T(8,128)S(1)}, f32[2048,3,64]{0,2,1:T(8,128)}, bf16[2048,3,64]{0,2,1:T(8,1...) while((s32[]{:T(128)}, f32[512,3,64]{0,2,1:T(8,128)S(1)}, ...), condition=%wide.region_30.31_spmd, body=%wide.region_29.30_spmd.sunk | while | flops 512461824 | bytes 19542320 | solution.py:162
  663.3 23.2 %while.118 = (s32[]{:T(128)}, f32[512,3,64]{0,2,1:T(8,128)}, f32[2048,3,64]{0,2,1:T(8,128)S(1)}, f32[2048,3,64]{0,2,1:T(8,128)}, bf16[2048,3,64]{0,2,1:T(8,128)(...) while((s32[]{:T(128)}, f32[512,3,64]{0,2,1:T(8,128)}, ...), condition=%wide.region_33.34_spmd, body=%wide.region_32.33_spmd.sunk | while | flops 512461824 | bytes 22663500 | solution.py:162
  687.3 30.9 %while.119 = (s32[]{:T(128)}, f32[512,3,64]{0,2,1:T(8,128)}, f32[2048,3,64]{0,2,1:T(8,128)S(1)}, f32[2048,3,64]{0,2,1:T(8,128)}, bf16[2048,3,64]{0,2,1:T(8,128)(...) while((s32[]{:T(128)}, f32[512,3,64]{0,2,1:T(8,128)}, ...), condition=%wide.region_36.37_spmd, body=%wide.region_35.36_spmd.sunk | while | flops 512461824 | bytes 22663500 | solution.py:162
  731.6 24.4 %reduce-scatter.13.cloned.1.call-done = bf16[2048,96]{0,1:T(8,128)(2,1)} async-done(((bf16[2048,384]{0,1:T(8,128)(2,1)}), bf16[2048,96]{0,1:T(8,128)(2,1)}) %reduce-scatter.13.cloned.1.call-update) | async-done | bytes 393232 | tf_op jit(solution)/shard_map/reduce_scatter | solution.py:279
  782.0 11.2 %reduce-scatter.17.cloned.1.call-done = bf16[2048,96]{0,1:T(8,128)(2,1)} async-done(((bf16[2048,384]{0,1:T(8,128)(2,1)}), bf16[2048,96]{0,1:T(8,128)(2,1)}) %reduce-scatter.17.cloned.1.call-update) | async-done | bytes 393232 | tf_op jit(solution)/shard_map/reduce_scatter | solution.py:282
  795.3 14.7 %all-reduce.1 = (f32[192]{0:T(256)}, f32[96]{0:T(128)}, f32[768]{0:T(1024)}) all-reduce(f32[192]{0:T(256)S(1)} %reduce_sum.251, f32[96]{0:T(128)S(1)} %convert_reduce_fusion.6, f32[768]{0:T(1024)S(1)} %copy-done.109), channel_id=1, replica_groups=mesh['dp'=8,'mp'=4] {'dp'}, use_global_device_ids=true, to_apply=%region_48.49 | all-reduce | flops 1056 | bytes 8448 | tf_op jit(solution)/shard_map/psum | solution.py:316
  810.0 44.6 %reduce-scatter.15.cloned.1.call-done = bf16[512,768]{1,0:T(8,128)(2,1)} async-done(((bf16[2048,768]{1,0:T(8,128)(2,1)}), bf16[512,768]{1,0:T(8,128)(2,1)}) %reduce-scatter.15.cloned.1.call-update) | async-done | bytes 786448 | tf_op jit(solution)/shard_map/reduce_scatter | solution.py:292
  858.4 41.5 %all-reduce = (f32[768]{0:T(1024)}, f32[768]{0:T(1024)}, f32[768]{0:T(1024)}, f32[768]{0:T(1024)}, f32[768]{0:T(1024)}, /*index=5*/f32[768]{0:T(1024)}) all-reduce(f32[768]{0:T(1024)S(1)} %get-tuple-element.454, f32[768]{0:T(1024)S(1)} %get-tuple-element.459, f32[768]{0:T(1024)S(1)} %copy-done.99, ...), channel_id=1, replica_groups=mesh['dp'=8,'mp'=4] {'dp','mp'}, use_global_device_ids=true, to_apply=%region_43.44 | all-reduce | flops 4608 | bytes 36864 | tf_op jit(solution)/shard_map/psum | solution.py:332
  903.6 67.2 %all-reduce.5.cloned.1.call-done = (f32[768,192]{0,1:T(8,128)}, f32[768,192]{0,1:T(8,128)}, f32[768,96]{0,1:T(8,128)}, f32[192,768]{1,0:T(8,128)}, f32[768,768]{1,0:T(8,128)}, /*index=5*/f32[768,768]{1,0:T(8,128)}) async-done(((f32[768,192]{0,1:T(8,128)}, f32[768,192]{0,1:T(8,128)}, f32[768,96]{0,1:T(8,128)}, f32[192,768]{1,0:T(8,128)}, f32[768,768]{1,0:T(8,128)}, /*index=5*/f32[768,768]{1,0:T(8,128)}), ...) | async-done | bytes 6782992 | tf_op jit(solution)/shard_map/psum | solution.py:316
  (615 shorter events, 269.7 us)
Async XLA Ops:
  7.2 417.5 %copy-start = (bf16[768,768]{1,0:T(8,128)(2,1)S(1)}, bf16[768,768]{1,0:T(8,128)(2,1)}, u32[]{:S(2)}) copy-start(bf16[768,768]{1,0:T(8,128)(2,1)} %param.51) | copy-start | bytes 3538948
  7.3 71.1 %all-gather.7.cloned.1.call-start = ((), (), s32[]{:S(2)}) async-start(), calls=%async_computation.6 | async-start | bytes 3932160 | tf_op jit(solution)/shard_map/all_gather | solution.py:197
  12.0 103.6 %all-gather.11.cloned.1.call-start = ((), (), s32[]{:S(2)}) async-start(), calls=%async_computation.8 | async-start | bytes 1966080 | tf_op jit(solution)/shard_map/all_gather | solution.py:210
  12.8 140.9 %all-gather.9.cloned.1.call-start = ((), (), s32[]{:S(2)}) async-start(), calls=%async_computation.7 | async-start | bytes 1966080 | tf_op jit(solution)/shard_map/all_gather | solution.py:209
  82.1 210.6 %reduce-scatter.7.cloned.1.call-start = ((), (), s32[]{:S(2)}) async-start(), calls=%async_computation.9 | async-start | bytes 3932160 | tf_op jit(solution)/shard_map/reduce_scatter | solution.py:223
  233.3 127.3 %all-gather.13.cloned.1.call-start = ((), (), s32[]{:S(2)}) async-start(), calls=%async_computation.10 | async-start | bytes 3932160 | tf_op jit(solution)/shard_map/all_gather | solution.py:232
  297.1 127.6 %all-gather.15.cloned.1.call-start = ((), (), s32[]{:S(2)}) async-start(), calls=%async_computation.12 | async-start | bytes 3932160 | tf_op jit(solution)/shard_map/all_gather | solution.py:233
  298.8 126.0 %copy-start.115 = (f32[768]{0:T(1024)S(1)}, f32[768]{0:T(1024)}, u32[]{:S(2)}) copy-start(f32[768]{0:T(1024)} %param.50) | copy-start | bytes 9220
  298.8 202.9 %reduce-scatter.11.cloned.1.call-start = ((), (), s32[]{:S(2)}) async-start(), calls=%async_computation.13 | async-start | bytes 3932160 | tf_op jit(solution)/shard_map/reduce_scatter | solution.py:252
  442.5 121.9 %reduce-scatter.9.cloned.1.call-start = ((), (), s32[]{:S(2)}) async-start(), calls=%async_computation.11 | async-start | bytes 3932160 | tf_op jit(solution)/shard_map/reduce_scatter | solution.py:239
  449.2 115.2 %copy-start.108 = (f32[768]{0:T(1024)S(1)}, f32[768]{0:T(1024)}, u32[]{:S(2)}) copy-start(f32[768]{0:T(1024)} %param.52) | copy-start | bytes 9220
  449.2 183.8 %all-gather.17.cloned.1.call-start = ((), (), s32[]{:S(2)}) async-start(), calls=%async_computation.14 | async-start | bytes 3932160 | tf_op jit(solution)/shard_map/all_gather | solution.py:260
  569.6 186.4 %reduce-scatter.13.cloned.1.call-start = ((), (), s32[]{:S(2)}) async-start(), calls=%async_computation.15 | async-start | bytes 1966080 | tf_op jit(solution)/shard_map/reduce_scatter | solution.py:279
  721.8 71.4 %reduce-scatter.17.cloned.1.call-start = ((), (), s32[]{:S(2)}) async-start(), calls=%async_computation.17 | async-start | bytes 1966080 | tf_op jit(solution)/shard_map/reduce_scatter | solution.py:282
  722.5 132.1 %reduce-scatter.15.cloned.1.call-start = ((), (), s32[]{:S(2)}) async-start(), calls=%async_computation.16 | async-start | bytes 3932160 | tf_op jit(solution)/shard_map/reduce_scatter | solution.py:292
  763.4 207.4 %all-reduce.5.cloned.1.call-start = ((), (), s32[]{:S(2)}) async-start(), calls=%async_computation.18 | async-start | bytes 13565952 | tf_op jit(solution)/shard_map/psum | solution.py:316
  781.8 72.8 %copy-start.81 = (f32[768]{0:T(1024)S(1)}, f32[768]{0:T(1024)}, u32[]{:S(2)}) copy-start(f32[768]{0:T(1024)} %param.38) | copy-start | bytes 9220
  781.9 74.5 %copy-start.93 = (f32[512]{0:T(512)S(1)}, f32[512]{0:T(512)}, u32[]{:S(2)}) copy-start(f32[512]{0:T(512)} %copy-done.92) | copy-start | bytes 6148
  781.9 74.5 %copy-start.87 = (f32[512]{0:T(512)S(1)}, f32[512]{0:T(512)}, u32[]{:S(2)}) copy-start(f32[512]{0:T(512)} %copy-done.86) | copy-start | bytes 6148
  782.0 76.4 %copy-start.96 = (f32[768]{0:T(1024)S(1)}, f32[768]{0:T(1024)}, u32[]{:S(2)}) copy-start(f32[768]{0:T(1024)} %get-tuple-element.640) | copy-start | bytes 9220
  782.0 76.5 %copy-start.97 = (f32[768]{0:T(1024)S(1)}, f32[768]{0:T(1024)}, u32[]{:S(2)}) copy-start(f32[768]{0:T(1024)} %get-tuple-element.456) | copy-start | bytes 9220
  782.0 76.5 %copy-start.98 = (f32[768]{0:T(1024)S(1)}, f32[768]{0:T(1024)}, u32[]{:S(2)}) copy-start(f32[768]{0:T(1024)} %get-tuple-element.458) | copy-start | bytes 9220
  782.0 76.5 %copy-start.99 = (f32[768]{0:T(1024)S(1)}, f32[768]{0:T(1024)}, u32[]{:S(2)}) copy-start(f32[768]{0:T(1024)} %get-tuple-element.642) | copy-start | bytes 9220
  782.0 118.0 %copy-start.91 = (f32[512]{0:T(512)S(1)}, f32[512]{0:T(512)}, u32[]{:S(2)}) copy-start(f32[512]{0:T(512)} %copy-done.90) | copy-start | bytes 6148
  (156 other events, 1505.8 us)
Sparse Core Ops, SparseCore 0:
  12.1 66.1 all-gather.6
  79.9 35.7 all-gather.10
  117.8 35.8 all-gather.8
  233.4 59.2 reduce-scatter.6
  297.2 63.3 all-gather.12
  362.6 62.0 all-gather.14
  442.6 59.0 reduce-scatter.10
  504.0 60.2 reduce-scatter.8
  569.7 63.3 all-gather.16
  721.9 34.0 reduce-scatter.12
  758.9 34.2 reduce-scatter.16
  795.3 59.2 reduce-scatter.14
  860.4 110.3 all-reduce.4
where the time goes:
time: 997 us; the launch traced here: 987 us
  waiting for transfers between devices  631 us (63%)
  matrix products  180 us (18%)
  other arithmetic  63.6 us (6%)
  blocking collectives  56.2 us (6%)
  local copies, waits for them, and re-layouts  36.4 us (4%)
  between operations  15.9 us (2%)
    psum x1, waiting for transfers between devices, shards(): lax.psum((grad_w_query, grad_b_query, grad_w_key, grad_w_value, grad_b_va...  67.2 us
    all_gather x1, waiting for transfers between devices, shards(): normed = lax.all_gather(normed_local, 'mp', axis=0, tiled=True)  65.5 us
    all_gather x1, waiting for transfers between devices, shards(): lax.all_gather(normed_mid_local, 'mp', axis=0, tiled=True)  61.8 us
    all_gather x1, waiting for transfers between devices, shards(): grad_attn_all = lax.all_gather(grad_attn, 'mp', axis=0, tiled=True)  61 us
    reduce_scatter x1, waiting for transfers between devices, shards(): lax.psum_scatter(product(piece, w_down).astype(jnp.bfloat16), 'mp', scatt...  60.2 us
    reduce_scatter x1, waiting for transfers between devices, shards(): lax.psum_scatter(product(piece, w_out).astype(jnp.bfloat16), 'mp', scatte...  59.4 us
    all_gather x1, waiting for transfers between devices, shards(): lax.all_gather(grad_down, 'mp', axis=0, tiled=True)  56.6 us
    reduce_scatter x1, waiting for transfers between devices, shards(): lax.psum_scatter(product_right_t(piece, w_up).astype(jnp.bfloat16), 'mp',...  52.5 us
  transfers between devices with their start and end apart: 13, of which 13 were waited for; matrix products, arithmetic and copies ran while one was open for 7% of the time, Pallas kernels for 0%

commit v1 on v0

v1 whole, which is shorter than its diff:
```python
import functools

import jax
import jax.numpy as jnp
from jax import lax
from jax.experimental import pallas as pl
from jax.experimental.pallas import tpu as pltpu
from jax.sharding import PartitionSpec as P

EPSILON = 1e-05
HEAD = 64
BLK = 256
LOG2E = 1.4426950408889634
LN2 = 0.6931471805599453


def nn(left, right):
    return lax.dot_general(left, right, (((1,), (0,)), ((), ())), preferred_element_type=jnp.float32)


def nt(left, right):
    return lax.dot_general(left, right, (((1,), (1,)), ((), ())), preferred_element_type=jnp.float32)


def tn(left, right):
    return lax.dot_general(left, right, (((0,), (0,)), ((), ())), preferred_element_type=jnp.float32)


def causal_mask(size):
    keys = lax.broadcasted_iota(jnp.int32, (size, size), 0)
    rows = lax.broadcasted_iota(jnp.int32, (size, size), 1)
    return keys <= rows


def forward_kernel(heads, factor, first_ref, q_ref, k_ref, v_ref, out_ref, lse_ref):
    row = pl.program_id(0)
    split = first_ref[0] // BLK
    lowest = jnp.where(row >= split, split, 0)
    query = [q_ref[h * HEAD : (h + 1) * HEAD, :] for h in range(heads)]

    def block(col, carry, masked):
        cols = pl.ds(pl.multiple_of(col * BLK, BLK), BLK)
        result = []
        for h in range(heads):
            run_max, run_sum, running = carry[h]
            band = slice(h * HEAD, (h + 1) * HEAD)
            scores = tn(k_ref[band, cols], query[h])
            if masked:
                scores = jnp.where(causal_mask(BLK), scores, -1e30)
            new_max = jnp.maximum(run_max, jnp.max(scores, 0, keepdims=True))
            change = jnp.exp2((run_max - new_max) * factor)
            weights = jnp.exp2((scores - new_max) * factor)
            run_sum = run_sum * change + jnp.sum(weights, 0, keepdims=True)
            running = running * change + nn(v_ref[band, cols], weights.astype(jnp.bfloat16))
            result.append((new_max, run_sum, running))
        return tuple(result)

    start = tuple(
        (
            jnp.full((1, BLK), -1e30, jnp.float32),
            jnp.zeros((1, BLK), jnp.float32),
            jnp.zeros((HEAD, BLK), jnp.float32),
        )
        for _ in range(heads)
    )
    start = block(row, start, True)
    final = lax.fori_loop(lowest, row, lambda col, carry: block(col, carry, False), start)
    for h in range(heads):
        run_max, run_sum, running = final[h]
        out_ref[0, h * HEAD : (h + 1) * HEAD, :] = (running / run_sum).astype(jnp.bfloat16)
        lse_ref[h : h + 1, :] = run_max * factor + jnp.log2(run_sum)


def attend_forward(first_length, queries, keys, values, parts):
    width, count = queries.shape
    heads = width // HEAD
    blocks = count // BLK
    chunk = count // parts
    per = chunk // BLK
    factor = HEAD ** (-0.5) * LOG2E
    spec_all = pl.BlockSpec((width, count), lambda i: (0, 0))
    return pl.pallas_call(
        functools.partial(forward_kernel, heads, factor),
        grid=(blocks,),
        in_specs=[
            pl.BlockSpec(memory_space=pltpu.SMEM),
            pl.BlockSpec((width, BLK), lambda i: (0, i)),
            spec_all,
            spec_all,
        ],
        out_specs=[
            pl.BlockSpec((1, width, BLK), lambda i: (i // per, 0, i % per)),
            pl.BlockSpec((8, BLK), lambda i: (0, i)),
        ],
        out_shape=[
            jax.ShapeDtypeStruct((parts, width, chunk), jnp.bfloat16),
            jax.ShapeDtypeStruct((8, count), jnp.float32),
        ],
        cost_estimate=pl.CostEstimate(
            flops=4 * count * count * 256 * heads, bytes_accessed=8 * width * count, transcendentals=0
        ),
        name="attend_forward",
    )(first_length, queries, keys, values)


def backward_kernel(
    heads, factor, total, per, first_ref, q_ref, k_ref, v_ref, go_ref, o_ref, lse_ref,
    gq_ref, gk_ref, gv_ref, gq_sum, delta_ref,
):
    col = pl.program_id(0)
    split = first_ref[0] // BLK
    last = jnp.where(col < split, split, total)

    @pl.when(col == 0)
    def _():
        gq_sum[...] = jnp.zeros_like(gq_sum)
        for part in range(total // per):
            for h in range(heads):
                band = slice(h * HEAD, (h + 1) * HEAD)
                both = go_ref[part, band, :].astype(jnp.float32) * o_ref[part, band, :].astype(jnp.float32)
                delta_ref[h : h + 1, part * per * BLK : (part + 1) * per * BLK] = jnp.sum(
                    both, 0, keepdims=True
                )

    bands = [slice(h * HEAD, (h + 1) * HEAD) for h in range(heads)]
    key = [k_ref[band, :] for band in bands]
    value = [v_ref[band, :] for band in bands]

    def block(row, carry, masked):
        rows = pl.ds(pl.multiple_of(row * BLK, BLK), BLK)
        inner = pl.ds(pl.multiple_of((row % per) * BLK, BLK), BLK)
        result = []
        for h in range(heads):
            grad_k, grad_v = carry[h]
            query = q_ref[bands[h], rows]
            grad_o = go_ref[row // per, bands[h], inner]
            scores = tn(key[h], query)
            probs = jnp.exp2(scores * factor - lse_ref[h : h + 1, rows])
            if masked:
                probs = jnp.where(causal_mask(BLK), probs, 0.0)
            grad_p = tn(value[h], grad_o)
            grad_s = (probs * (grad_p - delta_ref[h : h + 1, rows])).astype(jnp.bfloat16)
            grad_v = grad_v + nt(grad_o, probs.astype(jnp.bfloat16))
            grad_k = grad_k + nt(query, grad_s)
            gq_sum[bands[h], rows] += nn(key[h], grad_s)
            result.append((grad_k, grad_v))
        return tuple(result)

    zero = jnp.zeros((HEAD, BLK), jnp.float32)
    start = block(col, tuple((zero, zero) for _ in range(heads)), True)
    final = lax.fori_loop(col + 1, last, lambda row, carry: block(row, carry, False), start)
    scale = HEAD ** (-0.5)
    for h in range(heads):
        gk_ref[bands[h], :] = (final[h][0] * scale).astype(jnp.bfloat16)
        gv_ref[bands[h], :] = final[h][1].astype(jnp.bfloat16)

    @pl.when(col == total - 1)
    def _():
        gq_ref[...] = (gq_sum[...] * scale).astype(jnp.bfloat16)


def attend_backward(first_length, queries, keys, values, grad_context, context, lse):
    width, count = queries.shape
    heads = width // HEAD
    blocks = count // BLK
    parts, _, chunk = context.shape
    per = chunk // BLK
    factor = HEAD ** (-0.5) * LOG2E
    whole = lambda shape: pl.BlockSpec(shape, lambda i: (0,) * len(shape))
    one = pl.BlockSpec((width, BLK), lambda i: (0, i))
    flat = jax.ShapeDtypeStruct((width, count), jnp.bfloat16)
    return pl.pallas_call(
        functools.partial(backward_kernel, heads, factor, blocks, per),
        grid=(blocks,),
        in_specs=[
            pl.BlockSpec(memory_space=pltpu.SMEM),
            whole((width, count)),
            one,
            one,
            whole((parts, width, chunk)),
            whole((parts, width, chunk)),
            whole((8, count)),
        ],
        out_specs=[whole((width, count)), one, one],
        out_shape=[flat, flat, flat],
        scratch_shapes=[pltpu.VMEM((width, count), jnp.float32), pltpu.VMEM((8, count), jnp.float32)],
        cost_estimate=pl.CostEstimate(
            flops=10 * count * count * 256 * heads, bytes_accessed=14 * width * count, transcendentals=0
        ),
        name="attend_backward",
    )(first_length, queries, keys, values, grad_context, context, lse)


def layer_norm(values, gain, shift):
    center = values - jnp.mean(values, -1, keepdims=True)
    spread = jnp.mean(center * center, -1, keepdims=True)
    return center * lax.rsqrt(spread + EPSILON) * gain + shift


def gelu_tanh(values):
    return (
        0.5
        * values
        * (1.0 + jnp.tanh(0.7978845608028654 * (values + 0.044715 * values * values * values)))
    )


def shards(
    hidden_in,
    first_values,
    first_length,
    pre_gain,
    pre_shift,
    w_query,
    b_query,
    w_key,
    w_value,
    b_value,
    w_out,
    b_out,
    mid_gain,
    mid_shift,
    w_up,
    b_up,
    w_down,
    b_down,
    grad_out,
):
    bf16, f32 = jnp.bfloat16, jnp.float32
    rank = lax.axis_index("mp")
    parts = lax.axis_size("mp")
    copies = lax.axis_size("dp")
    copy = lax.axis_index("dp")
    width = w_query.shape[1]
    model = w_query.shape[0]
    hidden = w_up.shape[1]
    piece = w_value.shape[1]
    used = width // piece
    fresh_ranks = parts // used

    normed_local = layer_norm(hidden_in, pre_gain, pre_shift).astype(bf16)
    normed = lax.all_gather(normed_local, "mp", axis=0, tiled=True)
    count = normed.shape[0]
    chunk = count // parts

    fresh_moves, first_moves = [], []
    for which in range(used):
        fresh_moves.append([(d * used + which, d) for d in range(fresh_ranks)])
        first_moves.append([(d * used + which, d + fresh_ranks) for d in range(parts - fresh_ranks)])
    is_fresh = rank < fresh_ranks
    first_t = first_values.T
    first_own = jnp.concatenate([lax.ppermute(first_t, "mp", m) for m in first_moves], 0)
    w_value_own = jnp.concatenate([lax.ppermute(w_value, "mp", m) for m in fresh_moves], 1)
    b_value_row = b_value[None]
    b_value_own = jnp.concatenate([lax.ppermute(b_value_row, "mp", m) for m in fresh_moves], 1)[0]

    up_rows, out_rows = model // copies, width // copies
    mine = jnp.concatenate(
        [
            lax.dynamic_slice_in_dim(w_up, copy * up_rows, up_rows, 0),
            lax.dynamic_slice_in_dim(w_down, copy * (hidden // copies), hidden // copies, 0),
            lax.dynamic_slice_in_dim(w_out, copy * out_rows, out_rows, 0),
        ],
        0,
    )
    ranked = lax.all_gather(mine, "mp", axis=0)
    gathered = lax.all_gather(ranked, "dp", axis=0)
    down_rows = hidden // copies

    def whole(start, size):
        part = gathered[:, :, start : start + size]
        return jnp.transpose(part, (1, 0, 2, 3)).reshape(parts, copies * size, model)

    up_all = whole(0, up_rows)
    down_all = whole(up_rows, down_rows)
    out_all = whole(up_rows + down_rows, out_rows).reshape(parts * width, model)
    b_up_all = lax.all_gather(b_up, "mp", axis=0)

    queries = (tt(w_query, normed) + b_query[:, None]).astype(bf16)
    keys = tt(w_key, normed).astype(bf16)
    fresh = (tt(w_value_own, normed) + b_value_own[:, None]).astype(bf16)
    values = jnp.where(is_fresh, fresh, first_own)
    context, lse = attend_forward(first_length, queries, keys, values, parts)
    context_rows = lax.all_to_all(context, "mp", 0, 0, tiled=True).reshape(parts * width, chunk)
    middle = hidden_in + (tn(context_rows, out_all) + b_out)
    normed_mid = layer_norm(middle, mid_gain, mid_shift).astype(bf16)
    up_values = (
        lax.dot_general(
            normed_mid, up_all, (((1,), (1,)), ((), ())), preferred_element_type=f32
        )
        + b_up_all[None]
    )
    activated = gelu_tanh(up_values).astype(bf16)
    layer_out = middle + (
        lax.dot_general(
            activated, down_all, (((1, 2), (0, 1)), ((), ())), preferred_element_type=f32
        )
        + b_down
    )
    grad_down = grad_out.astype(bf16)
    grad_b_down = jnp.sum(grad_down.astype(f32), 0)
    grad_w_down = lax.dot_general(
        activated, grad_down, (((0,), (0,)), ((), ())), preferred_element_type=f32
    ).astype(bf16)
    grad_activated = lax.dot_general(
        grad_down, down_all, (((1,), (2,)), ((), ())), preferred_element_type=f32
    )
    _, gelu_pull = jax.vjp(gelu_tanh, up_values)
    grad_up = gelu_pull(grad_activated)[0].astype(bf16)
    grad_b_up = jnp.sum(grad_up.astype(f32), 0)
    grad_w_up = jnp.stack([tn(normed_mid, grad_up[:, j]) for j in range(parts)], 0).astype(bf16)
    grad_normed_mid = lax.dot_general(
        grad_up, up_all, (((1, 2), (0, 2)), ((), ())), preferred_element_type=f32
    )
    _, mid_pull = jax.vjp(layer_norm, middle, mid_gain, mid_shift)
    grad_mid_part, grad_mid_gain, grad_mid_shift = mid_pull(grad_normed_mid)
    grad_middle = grad_out + grad_mid_part
    grad_attn = grad_middle.astype(bf16)
    grad_b_out = jnp.sum(grad_attn.astype(f32), 0)
    grad_context_rows = nt(out_all, grad_attn).astype(bf16).reshape(parts, width, chunk)
    grad_context = lax.all_to_all(grad_context_rows, "mp", 0, 0, tiled=True)
    grad_w_out = nn(context_rows, grad_attn).astype(bf16).reshape(parts, width, model)

    def scatter(full, rows):
        return jnp.transpose(full.reshape(parts, copies, rows, model), (1, 0, 2, 3))

    partial = jnp.concatenate(
        [scatter(grad_w_up, up_rows), scatter(grad_w_down, down_rows), scatter(grad_w_out, out_rows)], 2
    )
    rows_each = partial.shape[2]
    reduced = lax.psum_scatter(
        partial.reshape(copies * parts * rows_each, model), "dp", scatter_dimension=0, tiled=True
    )
    reduced = lax.psum_scatter(reduced, "mp", scatter_dimension=0, tiled=True)
    summed = lax.all_gather(reduced, "dp", axis=0, tiled=True).reshape(copies, rows_each, model)

    def own(start, size):
        return summed[:, start : start + size].reshape(copies * size, model).astype(f32)

    g_w_up = own(0, up_rows)
    g_w_down = own(up_rows, down_rows)
    g_w_out = own(up_rows + down_rows, out_rows)

    grad_q, grad_k, grad_v = attend_backward(
        first_length, queries, keys, values, grad_context, context, lse
    )
    back_fresh = [[(d, s) for s, d in m] for m in fresh_moves]
    back_first = [[(d, s) for s, d in m] for m in first_moves]
    grad_first_t = sum(
        lax.ppermute(grad_v[i * piece : (i + 1) * piece], "mp", m) for i, m in enumerate(back_first)
    )
    grad_first = grad_first_t.T.astype(f32)
    grad_fresh = jnp.where(is_fresh, grad_v, jnp.zeros_like(grad_v))
    grad_normed = lax.psum_scatter(
        (tt_rows(grad_q, w_query) + tt_rows(grad_k, w_key) + tt_rows(grad_fresh, w_value_own)).astype(
            bf16
        ),
        "mp",
        scatter_dimension=0,
        tiled=True,
    ).astype(f32)
    g_q = tn_t(normed, grad_q)
    g_k = tn_t(normed, grad_k)
    g_v = tn_t(normed, grad_fresh).astype(bf16)
    g_v = sum(
        lax.ppermute(g_v[:, i * piece : (i + 1) * piece], "mp", m) for i, m in enumerate(back_fresh)
    )
    grad_b_query = jnp.sum(grad_q.astype(f32), 1)
    sums_v = jnp.sum(grad_fresh.astype(f32), 1)[None]
    grad_b_value = sum(
        lax.ppermute(sums_v[:, i * piece : (i + 1) * piece], "mp", m) for i, m in enumerate(back_fresh)
    )[0]
    grad_w_query, grad_w_key, grad_w_value = lax.psum((g_q.astype(bf16), g_k.astype(bf16), g_v), "dp")
    grad_b_query, grad_b_value = lax.psum((grad_b_query, grad_b_value), "dp")
    _, pre_pull = jax.vjp(layer_norm, hidden_in, pre_gain, pre_shift)
    grad_pre_part, grad_pre_gain, grad_pre_shift = pre_pull(grad_normed)
    grad_input = grad_middle + grad_pre_part
    vectors = lax.psum(
        jnp.stack(
            [grad_pre_gain, grad_pre_shift, grad_b_out, grad_mid_gain, grad_mid_shift, grad_b_down]
            + [grad_b_up[j] for j in range(parts)],
            0,
        ),
        ("dp", "mp"),
    )
    g_b_up = lax.dynamic_slice_in_dim(vectors[6:], rank, 1, 0)[0]
    return (
        layer_out,
        grad_input,
        grad_first,
        vectors[0],
        vectors[1],
        grad_w_query.astype(f32),
        grad_b_query,
        grad_w_key.astype(f32),
        grad_w_value.astype(f32),
        grad_b_value,
        g_w_out,
        vectors[2],
        vectors[3],
        vectors[4],
        g_w_up,
        g_b_up,
        g_w_down,
        vectors[5],
    )


def tt(weight, rows):
    return lax.dot_general(weight, rows, (((0,), (1,)), ((), ())), preferred_element_type=jnp.float32)


def tt_rows(grad_t, weight):
    return lax.dot_general(grad_t, weight, (((0,), (1,)), ((), ())), preferred_element_type=jnp.float32)


def tn_t(rows, grad_t):
    return lax.dot_general(rows, grad_t, (((0,), (1,)), ((), ())), preferred_element_type=jnp.float32)


def solution(mesh):
    placed = (
        P(("dp", "mp"), None),
        P("dp", "mp"),
        P("dp"),
        P(),
        P(),
        P(None, "mp"),
        P("mp"),
        P(None, "mp"),
        P(None, "mp"),
        P("mp"),
        P("mp", None),
        P(),
        P(),
        P(),
        P(None, "mp"),
        P("mp"),
        P("mp", None),
        P(),
        P(("dp", "mp"), None),
    )
    return jax.shard_map(
        shards,
        mesh=mesh,
        in_specs=placed,
        out_specs=(
            P(("dp", "mp"), None),
            P(("dp", "mp"), None),
            P("dp", "mp"),
            P(),
            P(),
            P(None, "mp"),
            P("mp"),
            P(None, "mp"),
            P(None, "mp"),
            P("mp"),
            P("mp", None),
            P(),
            P(),
            P(),
            P(None, "mp"),
            P("mp"),
            P("mp", None),
            P(),
        ),
        check_vma=False,
    )
```

time: 997 us -> 578 us (0.58)
  waiting for transfers between devices: 631 us -> 234 us
  matrix products: 180 us -> 72.8 us
  Pallas kernels: 0 us -> 74.1 us
  other arithmetic: 63.6 us -> 23.3 us
  starting transfers between devices: 1.15 us -> 41.2 us
  blocking collectives: 56.2 us -> 72.9 us
    all_gather x5 -> x3, waiting for transfers between devices: 245 us -> 32.8 us  [the longest x1 32.8 us: shards(): ranked = lax.all_gather(mine, 'mp', axis=0)]
    reduce_scatter x6 -> x3, waiting for transfers between devices: 252 us -> 132 us  [the longest x1 74.4 us: shards(): lax.psum_scatter(partial.reshape(copies * parts * rows_each, model), 'dp'...]
    dot_general x88 -> x21, matrix products: 180 us -> 72.8 us  [the longest x3 15.1 us: tt_rows(): lax.dot_general(grad_t, weight, (((0,), (1,)), ((), ())), preferred_eleme...]
    pallas_call x0 -> x2, Pallas kernels: none -> 74.1 us  [the longest x1 37.3 us: attend_forward(): pl.pallas_call(functools.partial(forward_kernel, heads, factor), grid=(bl...]
    psum x1, waiting for transfers between devices: 67.2 us -> 11.2 us  [shards(): lax.psum((g_q.astype(bf16), g_k.astype(bf16), g_v), 'dp')]
    ppermute x0 -> x12, starting transfers between devices: none -> 24 us  [the longest x2 7.86 us: shards(): lax.ppermute(first_t, 'mp', m)]
    all_gather x0 -> x1, blocking collectives: none -> 19.1 us  [shards(): b_up_all = lax.all_gather(b_up, 'mp', axis=0)]
    all_to_all x0 -> x2, starting transfers between devices: none -> 16.8 us  [the longest x1 12.7 us: shards(): lax.all_to_all(context, 'mp', 0, 0, tiled=True)]
  transfers between devices with their start and end apart: 13 -> 22, of which waited for: 13 -> 7; matrix products, arithmetic and copies ran while one was open for 7% -> 13% of each run, Pallas kernels for 0% -> 13%
where the time goes in v1:
time: 578 us; the launch traced here: 566 us
  waiting for transfers between devices  234 us (40%)
  Pallas kernels  74.1 us (13%)
  blocking collectives  72.9 us (13%)
  matrix products  72.8 us (13%)
  starting transfers between devices  41.2 us (7%)
  local copies, waits for them, and re-layouts  32.2 us (6%)
  other arithmetic  23.3 us (4%)
  between operations  16 us (3%)
    reduce_scatter x1, waiting for transfers between devices, shards(): lax.psum_scatter(partial.reshape(copies * parts * rows_each, model), 'dp'...  74.4 us
    reduce_scatter x1, waiting for transfers between devices, shards(): lax.psum_scatter((tt_rows(grad_q, w_query) + tt_rows(grad_k, w_key) + tt_...  57.7 us
    all_gather x1, waiting for transfers between devices, shards(): normed = lax.all_gather(normed_local, 'mp', axis=0, tiled=True)  55.8 us
    psum x1, blocking collectives, shards(): lax.psum(jnp.stack([grad_pre_gain, grad_pre_shift, grad_b_out, grad_mid_g...  40.7 us
    pallas_call x1, Pallas kernels, attend_forward(): pl.pallas_call(functools.partial(forward_kernel, heads, factor), grid=(bl...  37.3 us
    pallas_call x1, Pallas kernels, attend_backward(): pl.pallas_call(functools.partial(backward_kernel, heads, factor, blocks,...  36.8 us
    all_gather x1, waiting for transfers between devices, shards(): ranked = lax.all_gather(mine, 'mp', axis=0)  32.8 us
    all_gather x1, blocking collectives, shards(): b_up_all = lax.all_gather(b_up, 'mp', axis=0)  19.1 us
  transfers between devices with their start and end apart: 22, of which 7 were waited for; matrix products, arithmetic and copies ran while one was open for 13% of the time, Pallas kernels for 13%

profile of v1, /device:TPU:0, one launch (start us, length us, event | category | flops | bytes accessed | tf_op | source)
XLA Modules:
  0.0 566.3 jit_solution(15746716793832607247)
XLA Ops:
  13.0 32.8 %all-gather.13.cloned.1.call-done = bf16[864,768]{1,0:T(8,128)(2,1)} async-done(((bf16[216,768]{1,0:T(8,128)(2,1)}), bf16[864,768]{1,0:T(8,128)(2,1)}) %all-gather.13.cloned.1.call-update) | async-done | bytes 1327120 | tf_op jit(solution)/shard_map/all_gather | solution.py:266
  51.9 7.2 %collective-permute-start.4 = (bf16[96,2048]{1,0:T(8,128)(2,1)S(1)}, bf16[96,2048]{1,0:T(8,128)(2,1)}, u32[]{:S(2)}, u32[]{:S(2)}) collective-permute-start(bf16[96,2048]{1,0:T(8,128)(2,1)S(1)} %bitcast.172), channel_id=1, source_target_pairs={{0,2},{2,3},{4,6},{6,7},{8,10},{10,11},{12,14},{14,15},{16,18},{18... | collective-permute-start | bytes 1179656 | tf_op jit(solution)/shard_map/ppermute | solution.py:252
  59.2 55.8 %all-gather.9.cloned.1.call-done = bf16[2048,768]{1,0:T(8,128)(2,1)} async-done(((bf16[512,768]{1,0:T(8,128)(2,1)}), bf16[2048,768]{1,0:T(8,128)(2,1)}) %all-gather.9.cloned.1.call-update) | async-done | bytes 3145744 | tf_op jit(solution)/shard_map/all_gather | solution.py:242
  115.1 4.1 fusion.12.k_ref
  124.3 37.3 %attend_forward.1 = (bf16[4,192,512]{2,1,0:T(8,128)(2,1)}, f32[8,2048]{1,0:T(8,128)}) custom-call(s32[1]{0:T(128)S(6)} %copy.67.first_ref, bf16[192,2048]{1,0:T(8,128)(2,1)} %fusion.11.q_ref, bf16[192,2048]{1,0:T(8,128)(2,1)} %fusion.12.k_ref, bf16[192,2048]{1,0:T(8,128)(2,1)} %fusion.13.v_ref), custom_call_target="tpu_custom_call" | custom-call | flops 12884901888 | bytes 3145728 | tf_op jit(solution)/shard_map/attend_forward/pallas_call | solution.py:82
  161.6 12.7 %all-to-all-start = ((bf16[4,192,512]{2,1,0:T(8,128)(2,1)}), bf16[4,192,512]{2,1,0:T(8,128)(2,1)}, u32[]{:S(2)}, u32[]{:S(2)}) async-start(bf16[4,192,512]{2,1,0:T(8,128)(2,1)} %get-tuple-element.23.o_ref), calls=%async_computation | async-start | bytes 1572864 | tf_op jit(solution)/shard_map/all_to_all | solution.py:284
  174.3 19.1 %all-gather.3 = f32[4,1,768]{2,1,0:T(1,128)S(1)} all-gather(f32[1,1,768]{2,1,0:T(1,128)S(1)} %reshape.192), channel_id=4, replica_groups=mesh['dp'=8,'mp'=4] {'mp'}, dimensions={0}, use_global_device_ids=true | all-gather | bytes 15360 | tf_op jit(solution)/shard_map/all_gather | solution.py:277
  193.4 6.8 %slice_bitcast_fusion.1 = (bf16[4,8,96,768]{3,2,0,1:T(8,128)(2,1)S(1)}, bf16[4,8,96,768]{3,2,0,1:T(8,128)(2,1)}) fusion(bf16[8,4,216,768]{3,2,1,0:T(8,128)(2,1)} %bitcast.144), kind=kLoop, calls=%fused_computation.20 | loop fusion | bytes 18874368 | tf_op jit(solution)/shard_map/transpose | solution.py:272
  207.0 3.4 copy.55
  213.7 5.7 %convolution_convert_fusion = bf16[4,768,768]{2,1,0:T(8,128)(2,1)} fusion(f32[512,768]{1,0:T(8,128)S(1)} %copy-done.9, f32[512,4,768]{2,0,1:T(8,128)S(1)} %fusion.26, f32[4,768]{1,0:T(4,128)S(1)} %bitcast.166), kind=kOutput, calls=%fused_computation.22 | convolution fusion | flops 2434400256 | bytes 12595200 | tf_op jit(solution)/shard_map/dot_general | solution.py:302
  219.4 7.6 %convert_reduce_fusion = (f32[4,768]{1,0:T(4,128)S(1)}, bf16[512,4,768]{2,0,1:T(8,128)(2,1)S(1)}) fusion(bf16[4,768,768]{2,1,0:T(8,128)(2,1)S(1)} %bitcast.146, f32[512,768]{1,0:T(8,128)S(1)} %copy-done.9, f32[512,4,768]{2,0,1:T(8,128)S(1)} %fusion.26, f32[4,768]{1,0:T(4,128)S(1)} %bitcast.167), kind=kOutput, calls=%fused_computation.16 | convolution fusion | flops 2458776576 | bytes 15753216 | tf_op jit(solution)/shard_map/dot_general | solution.py:305
  245.7 4.7 copy.58
  253.6 4.2 all-to-all-start.1
  257.8 74.4 %reduce-scatter.6.cloned.1.call-done = bf16[864,768]{1,0:T(8,128)(2,1)} async-done(((bf16[6912,768]{1,0:T(8,128)(2,1)}), bf16[864,768]{1,0:T(8,128)(2,1)}) %reduce-scatter.6.cloned.1.call-update) | async-done | bytes 1327120 | tf_op jit(solution)/shard_map/reduce_scatter | solution.py:331
  332.3 36.8 %attend_backward.1 = (bf16[192,2048]{1,0:T(8,128)(2,1)}, bf16[192,2048]{1,0:T(8,128)(2,1)}, bf16[192,2048]{1,0:T(8,128)(2,1)}) custom-call(s32[1]{0:T(128)S(6)} %copy.67.first_ref, bf16[192,2048]{1,0:T(8,128)(2,1)} %fusion.11.q_ref, bf16[192,2048]{1,0:T(8,128)(2,1)} %fusion.12.k_ref, bf16[192,2048]{1,0:T(8,128)(2,1)} %fusion.13.v_ref, ...), custom_call_target="tpu_custom_call" | custom-call | flops 32212254720 | bytes 5505024 | tf_op jit(solution)/shard_map/attend_backward/pallas_call | solution.py:172
  377.9 3.7 fusion.47
  381.6 3.6 fusion.46
  387.5 7.7 %add_convert_fusion = bf16[2048,768]{1,0:T(8,128)(2,1)} fusion(f32[2048,768]{1,0:T(8,128)} %fusion.46, f32[2048,768]{1,0:T(8,128)} %fusion.47, bf16[768,192]{0,1:T(8,128)(2,1)} %copy-done.17, bf16[192,2048]{1,0:T(8,128)(2,1)} %get-tuple-element.27, pred[]{:T(512)S(6)} %lt.13), kind=kOutput, calls=%fused_computation.17 | convolution fusion | flops 609091584 | bytes 16809984 | tf_op jit(solution)/shard_map/dot_general | solution.py:414
  396.1 9.9 %fusion.19 = f32[512,768]{1,0:T(8,128)} fusion(f32[512,768]{1,0:T(8,128)} %copy-done.8, bf16[4,768,768]{2,1,0:T(8,128)(2,1)} %bitcast.147, f32[768]{0:T(1024)S(1)} %copy-done.35, f32[512,4,768]{2,0,1:T(8,128)} %copy-done.40, f32[4,768]{1,0:T(4,128)S(1)} %bitcast.168), kind=kOutput, calls=%fused_computation.45 | convolution fusion | flops 2432434176 | bytes 14171136 | tf_op jit(solution)/shard_map/dot_general | solution.py:295
  410.0 4.8 collective-permute-start.11
  416.1 13.0 %all-reduce = (f32[192]{0:T(256)}, f32[96]{0:T(128)}) all-reduce(f32[192]{0:T(256)S(1)} %convert_reduce_fusion.3, f32[96]{0:T(128)S(1)} %add_bitcast_fusion), channel_id=1, replica_groups=mesh['dp'=8,'mp'=4] {'dp'}, use_global_device_ids=true, to_apply=%region_19.20 | all-reduce | flops 288 | bytes 2304 | tf_op jit(solution)/shard_map/psum | solution.py:374
  431.1 11.2 %all-reduce.4.cloned.1.call-done = (bf16[768,192]{0,1:T(8,128)(2,1)}, bf16[768,192]{0,1:T(8,128)(2,1)}, bf16[768,96]{0,1:T(8,128)(2,1)}) async-done(((bf16[768,192]{0,1:T(8,128)(2,1)}, bf16[768,192]{0,1:T(8,128)(2,1)}, bf16[768,96]{0,1:T(8,128)(2,1)}), (bf16[768,192]{0,1:T(8,128)(2,1)}, bf16[768,192]{0,1:T(8,128)(2,1)}, bf16[768,96]{0,1:T(8,128)(2,1)})) %all-reduce.4.cloned.1.call-update) | async-done | bytes 737296 | tf_op jit(solution)/shard_map/psum | solution.py:373
  447.6 57.7 %reduce-scatter.4.cloned.1.call-done = bf16[512,768]{1,0:T(8,128)(2,1)} async-done(((bf16[2048,768]{1,0:T(8,128)(2,1)}), bf16[512,768]{1,0:T(8,128)(2,1)}) %reduce-scatter.4.cloned.1.call-update) | async-done | bytes 786448 | tf_op jit(solution)/shard_map/reduce_scatter | solution.py:354
  510.1 40.7 %psum.42 = f32[10,768]{1,0:T(8,128)S(1)} all-reduce(f32[10,768]{1,0:T(8,128)S(1)} %stack.11), channel_id=1, replica_groups=mesh['dp'=8,'mp'=4] {'dp','mp'}, use_global_device_ids=true, to_apply=%region_16.17 | all-reduce | flops 7680 | bytes 61440 | tf_op jit(solution)/shard_map/psum | solution.py:378
  (206 shorter events, 85.3 us)
Async XLA Ops:
  7.2 107.9 %copy-start = (bf16[768,192]{0,1:T(8,128)(2,1)S(1)}, bf16[768,192]{0,1:T(8,128)(2,1)}, u32[]{:S(2)}) copy-start(bf16[768,192]{0,1:T(8,128)(2,1)} %param.26) | copy-start | bytes 884740
  7.2 38.5 %all-gather.13.cloned.1.call-start = ((), (), s32[]{:S(2)}) async-start(), calls=%async_computation.10 | async-start | bytes 1658880 | tf_op jit(solution)/shard_map/all_gather | solution.py:266
  10.0 105.1 %all-gather.9.cloned.1.call-start = ((), (), s32[]{:S(2)}) async-start(), calls=%async_computation.5 | async-start | bytes 3932160 | tf_op jit(solution)/shard_map/all_gather | solution.py:242
  12.9 180.5 %all-gather.15.cloned.1.call-start = ((), (), s32[]{:S(2)}) async-start(), calls=%async_computation.11 | async-start | bytes 11943936 | tf_op jit(solution)/shard_map/all_gather | solution.py:267
  45.8 13.4 %collective-permute-start = (bf16[768,96]{0,1:T(8,128)(2,1)S(1)}, bf16[768,96]{0,1:T(8,128)(2,1)S(1)}, u32[]{:S(2)}, u32[]{:S(2)}) collective-permute-start(bf16[768,96]{0,1:T(8,128)(2,1)S(1)} %copy-done.33), channel_id=1, source_target_pairs={{0,0},{2,1},{4,4},{6,5},{8,8},{10,9},{12,12},{14,13},{16,16},{18,1... | collective-permute-start | bytes 442376 | tf_op jit(solution)/shard_map/ppermute | solution.py:253
  46.4 5.5 collective-permute-start.3
  47.7 11.3 %collective-permute-start.2 = (f32[1,96]{1,0:T(1,128)S(1)}, f32[1,96]{1,0:T(1,128)S(1)}, u32[]{:S(2)}, u32[]{:S(2)}) collective-permute-start(f32[1,96]{1,0:T(1,128)S(1)} %bitcast.174), channel_id=1, source_target_pairs={{0,0},{2,1},{4,4},{6,5},{8,8},{10,9},{12,12},{14,13},{16,16},{18,1... | collective-permute-start | bytes 1160 | tf_op jit(solution)/shard_map/ppermute | solution.py:255
  48.4 10.8 %collective-permute-start.1 = (bf16[768,96]{0,1:T(8,128)(2,1)S(1)}, bf16[768,96]{0,1:T(8,128)(2,1)S(1)}, u32[]{:S(2)}, u32[]{:S(2)}) collective-permute-start(bf16[768,96]{0,1:T(8,128)(2,1)S(1)} %copy-done.33), channel_id=1, source_target_pairs={{1,0},{3,1},{5,4},{7,5},{9,8},{11,9},{13,12},{15,13},{17,16},{19,1... | collective-permute-start | bytes 442376 | tf_op jit(solution)/shard_map/ppermute | solution.py:253
  49.7 71.5 %collective-permute-start.5 = (bf16[96,2048]{1,0:T(8,128)(2,1)S(1)}, bf16[96,2048]{1,0:T(8,128)(2,1)S(1)}, u32[]{:S(2)}, u32[]{:S(2)}) collective-permute-start(bf16[96,2048]{1,0:T(8,128)(2,1)S(1)} %bitcast.171), channel_id=1, source_target_pairs={{1,2},{3,3},{5,6},{7,7},{9,10},{11,11},{13,14},{15,15},{17,18},{19... | collective-permute-start | bytes 1179656 | tf_op jit(solution)/shard_map/ppermute | solution.py:252
  51.9 69.3 %collective-permute-start.4 = (bf16[96,2048]{1,0:T(8,128)(2,1)S(1)}, bf16[96,2048]{1,0:T(8,128)(2,1)}, u32[]{:S(2)}, u32[]{:S(2)}) collective-permute-start(bf16[96,2048]{1,0:T(8,128)(2,1)S(1)} %bitcast.172), channel_id=1, source_target_pairs={{0,2},{2,3},{4,6},{6,7},{8,10},{10,11},{12,14},{14,15},{16,18},{18... | collective-permute-start | bytes 1179656 | tf_op jit(solution)/shard_map/ppermute | solution.py:252
  161.6 42.5 %all-to-all-start = ((bf16[4,192,512]{2,1,0:T(8,128)(2,1)}), bf16[4,192,512]{2,1,0:T(8,128)(2,1)}, u32[]{:S(2)}, u32[]{:S(2)}) async-start(bf16[4,192,512]{2,1,0:T(8,128)(2,1)} %get-tuple-element.23.o_ref), calls=%async_computation | async-start | bytes 1572864 | tf_op jit(solution)/shard_map/all_to_all | solution.py:284
  174.3 158.0 %reduce-scatter.6.cloned.1.call-start = ((), (), s32[]{:S(2)}) async-start(), calls=%async_computation.7 | async-start | bytes 11943936 | tf_op jit(solution)/shard_map/reduce_scatter | solution.py:331
  253.6 78.8 %all-to-all-start.1 = ((bf16[4,192,512]{2,1,0:T(8,128)(2,1)}), bf16[4,192,512]{2,1,0:T(8,128)(2,1)}, u32[]{:S(2)}, u32[]{:S(2)}) async-start(bf16[4,192,512]{2,1,0:T(8,128)(2,1)} %bitcast.161), calls=%async_computation.1 | async-start | bytes 1572864 | tf_op jit(solution)/shard_map/all_to_all | solution.py:321
  257.8 137.6 %reduce-scatter.8.cloned.1.call-start = ((), (), s32[]{:S(2)}) async-start(), calls=%async_computation.8 | async-start | bytes 1658880 | tf_op jit(solution)/shard_map/reduce_scatter | solution.py:334
  332.3 110.0 %all-reduce.4.cloned.1.call-start = ((), (), s32[]{:S(2)}) async-start(), calls=%async_computation.12 | async-start | bytes 1474560 | tf_op jit(solution)/shard_map/psum | solution.py:373
  372.3 14.5 %collective-permute-start.9 = (bf16[768,96]{0,1:T(8,128)(2,1)S(1)}, bf16[768,96]{0,1:T(8,128)(2,1)S(1)}, u32[]{:S(2)}, u32[]{:S(2)}) collective-permute-start(bf16[768,96]{0,1:T(8,128)(2,1)S(1)} %get-tuple-element.59), channel_id=1, source_target_pairs={{0,1},{1,3},{4,5},{5,7},{8,9},{9,11},{12,13},{13,15},{16,17},{17,1... | collective-permute-start | bytes 442376 | tf_op jit(solution)/shard_map/ppermute | solution.py:366
  375.7 11.1 %collective-permute-start.8 = (bf16[768,96]{0,1:T(8,128)(2,1)S(1)}, bf16[768,96]{0,1:T(8,128)(2,1)S(1)}, u32[]{:S(2)}, u32[]{:S(2)}) collective-permute-start(bf16[768,96]{0,1:T(8,128)(2,1)S(1)} %get-tuple-element.60), channel_id=1, source_target_pairs={{0,0},{1,2},{4,4},{5,6},{8,8},{9,10},{12,12},{13,14},{16,16},{17,1... | collective-permute-start | bytes 442376 | tf_op jit(solution)/shard_map/ppermute | solution.py:366
  387.5 117.8 %reduce-scatter.4.cloned.1.call-start = ((), (), s32[]{:S(2)}) async-start(), calls=%async_computation.6 | async-start | bytes 3932160 | tf_op jit(solution)/shard_map/reduce_scatter | solution.py:354
  395.3 156.8 %all-gather.11.cloned.1.call-start = ((), (), s32[]{:S(2)}) async-start(), calls=%async_computation.9 | async-start | bytes 2985984 | tf_op jit(solution)/shard_map/all_gather | solution.py:335
  406.9 22.1 %collective-permute-start.7 = (bf16[96,2048]{1,0:T(8,128)(2,1)}, bf16[96,2048]{1,0:T(8,128)(2,1)}, u32[]{:S(2)}, u32[]{:S(2)}) collective-permute-start(bf16[96,2048]{1,0:T(8,128)(2,1)} %get-tuple-element.57), channel_id=1, source_target_pairs={{2,1},{3,3},{6,5},{7,7},{10,9},{11,11},{14,13},{15,15},{18,17},{19... | collective-permute-start | bytes 1179656 | tf_op jit(solution)/shard_map/ppermute | solution.py:350
  408.4 20.7 %collective-permute-start.6 = (bf16[96,2048]{1,0:T(8,128)(2,1)}, bf16[96,2048]{1,0:T(8,128)(2,1)}, u32[]{:S(2)}, u32[]{:S(2)}) collective-permute-start(bf16[96,2048]{1,0:T(8,128)(2,1)} %get-tuple-element.58), channel_id=1, source_target_pairs={{2,0},{3,2},{6,4},{7,6},{10,8},{11,10},{14,12},{15,14},{18,16},{19... | collective-permute-start | bytes 1179656 | tf_op jit(solution)/shard_map/ppermute | solution.py:350
  409.9 95.4 %copy-start.21 = (f32[512]{0:T(512)S(1)}, f32[512]{0:T(512)}, u32[]{:S(2)}) copy-start(f32[512]{0:T(512)} %copy-done.20) | copy-start | bytes 6148
  410.0 6.1 %collective-permute-start.11 = (f32[1,96]{1,0:T(1,128)S(1)}, f32[1,96]{1,0:T(1,128)S(1)}, u32[]{:S(2)}, u32[]{:S(2)}) collective-permute-start(f32[1,96]{1,0:T(1,128)S(1)} %get-tuple-element.61), channel_id=1, source_target_pairs={{0,1},{1,3},{4,5},{5,7},{8,9},{9,11},{12,13},{13,15},{16,17},{17,1... | collective-permute-start | bytes 1160 | tf_op jit(solution)/shard_map/ppermute | solution.py:371
  414.8 1.3 collective-permute-start.10
  (43 other events, 725.1 us)
Sparse Core Ops, SparseCore 0:
  10.2 35.5 all-gather.12
  47.9 67.1 all-gather.8
  117.0 72.4 all-gather.14
  250.5 81.6 reduce-scatter.5
  334.4 31.7 reduce-scatter.7
  387.6 54.6 all-reduce.3
  444.6 60.6 reduce-scatter.3
  507.2 30.1 all-gather.10
